TPU v7x, 32 devices: a whole 2x2x4 slice. The times are simulated.
32 devices in a mesh: io: 8 (over z, y), cmp: 4 (over x, core).
Axes of the slice: x: 2, y: 2, z: 4, core: 2. Of those that a mesh axis runs over, the one named last changes fastest.
Arguments:
- fields: float32 [6, 8, 512, 4096], P(None, None, 'cmp', 'io'), may hold values from -6 to 6
- mean_old: float32 [6, 8, 512, 3072], P(None, 'cmp', 'io'), may hold values from -6 to 6
- land_mask: int32 [8, 512, 4096], P('cmp', 'io'), may hold values from 0 to 1, as said below
Outputs:
- mean_new: float32 [6, 8, 512, 3072], P(None, 'cmp', 'io')
- level_rms: float32 [6, 8], P(None, 'cmp')
Inputs may be any that keep to these rules, and one draw needn't show every extreme that they name: `land_mask`: each row (level, latitude) has between 1 and 3072 ocean points, and some row has exactly 3072.
All inputs are finite; a program needn't handle non-finite values.
Results may differ from a plain program's by a relative error of at most 0.00002.
Values sent between devices are 32-bit elements; how exact they have to be, the bound alone decides.
A program may use at most 128 MiB of HBM per device.

v0:
```python
import jax
import jax.numpy as jnp
from jax import lax
from jax.sharding import PartitionSpec as P

STEPS = 3


def move_left(array, amount):
    tail = jnp.zeros(array.shape[:-1] + (amount,), array.dtype)
    return jnp.concatenate([array[..., amount:], tail], axis=-1)


def pack_block(banded, land_mask):
    ncol = banded.shape[-1]
    width_out = 3 * ncol // 4
    ocean = land_mask == 1
    before = jnp.cumsum(1 - land_mask, axis=-1)
    offset = jnp.where(ocean, before, 0)
    values = jnp.where(ocean[None], banded, jnp.float32(0.0))
    present = ocean
    section = 0
    while 1 << section < ncol:
        amount = 1 << section
        moving = present & (offset >> section & 1 == 1)
        staying = present & jnp.logical_not(moving)
        arrive = move_left(moving.astype(jnp.int32), amount) == 1
        values = jnp.where(
            arrive[None],
            move_left(values, amount),
            jnp.where(staying[None], values, jnp.float32(0.0)),
        )
        offset = jnp.where(arrive, move_left(offset, amount), jnp.where(staying, offset, 0))
        present = arrive | staying
        section = section + 1
    return values[..., :width_out]


def on_device(fields, mean_old, land_mask):
    width_out = mean_old.shape[-1]
    banded = lax.all_to_all(
        lax.all_to_all(fields, "cmp", split_axis=1, concat_axis=2, tiled=True),
        "io",
        split_axis=2,
        concat_axis=3,
        tiled=True,
    )
    packed = pack_block(banded, land_mask)
    counts = jnp.sum(land_mask, axis=-1)
    in_row = jnp.arange(width_out, dtype=jnp.int32)[None, None, :] < counts[:, :, None]
    mean_new = jnp.where(
        in_row[None], (STEPS * mean_old + packed) / (STEPS + 1.0), jnp.float32(0.0)
    )
    square_sum = jnp.sum(mean_new * mean_new, axis=(2, 3))
    ocean_total = jnp.sum(counts, axis=1).astype(jnp.float32)
    square_all, total_all = lax.psum((square_sum, ocean_total), "io")
    level_rms = jnp.sqrt(square_all / total_all[None, :] + 1e-06)
    return (mean_new, level_rms)


def solution(mesh):
    in_specs = (P(None, None, "cmp", "io"), P(None, "cmp", "io", None), P("cmp", "io", None))
    out_specs = (P(None, "cmp", "io", None), P(None, "cmp"))
    return jax.shard_map(
        on_device, mesh=mesh, in_specs=in_specs, out_specs=out_specs, check_vma=False
    )
```

profile of v0, /device:TPU:0, one launch (start us, length us, event | category | flops | bytes accessed | tf_op | source)
XLA Modules:
  0.0 809.7 jit_solution(11888663161538195555)
XLA Ops:
  0.6 11.8 %copy.13 = f32[6,8,128,512]{3,2,0,1:T(8,128)} copy(f32[6,8,128,512]{3,2,1,0:T(8,128)} %param.3) | data formatting | bytes 25165824 | tf_op args[0]
  12.4 148.0 %all_to_all.36 = f32[6,8,128,512]{3,2,0,1:T(8,128)} all-to-all(f32[6,8,128,512]{3,2,0,1:T(8,128)} %copy.13), channel_id=1, replica_groups=mesh['io'=8,'cmp'=4] {'cmp'}, dimensions={1} | all-to-all | bytes 25165824 | tf_op jit(solution)/shard_map/all_to_all | solution.py:42
  160.4 11.8 %copy.15 = f32[6,2,4,128,512]{4,3,2,1,0:T(8,128)} copy(f32[6,2,4,128,512]{4,3,0,1,2:T(8,128)} %bitcast.20) | data formatting | bytes 25165824 | tf_op jit(solution)/shard_map/all_to_all | solution.py:42
  172.2 22.1 %copy.16 = f32[6,2,512,512]{3,1,0,2:T(2,128)} copy(f32[6,2,512,512]{3,2,1,0:T(8,128)} %bitcast.21) | data formatting | bytes 25165824 | tf_op jit(solution)/shard_map/all_to_all | solution.py:42
  194.3 7.3 all-to-all-start.1
  202.2 1.7 copy.23
  203.9 64.4 %reduce-window.6 = s32[2,64,32,128]{3,2,1,0:T(8,128)S(1)} reduce-window(s32[2,64,32,128]{3,2,1,0:T(8,128)} %bitcast.26, s32[]{:T(128)} %constant.17.clone.1), window={size=1x1x1x128 pad=0_0x0_0x0_0x127_0}, to_apply=%region_1.2 | reduce-window | flops 66584576 | bytes 4194308 | tf_op jit(solution)/shard_map/reduce-window
  268.3 1.9 slice.164
  270.2 2.4 copy.20
  273.0 1.7 broadcast_add_fusion
  274.7 2.9 reduce_window_sum.16
  277.6 2.4 fusion.3
  280.0 0.6 slice.166
  281.2 1.4 fusion.4
  282.6 0.6 slice.168
  283.8 2.5 fusion.5
  286.3 0.6 slice.170
  287.6 2.5 fusion.6
  290.1 0.6 slice.172
  291.3 2.7 fusion.7
  294.0 0.6 slice.174
  295.2 2.5 fusion.8
  297.7 0.6 slice.176
  298.9 2.5 fusion.9
  302.7 2.5 fusion.10
  306.0 2.5 fusion.11
  308.7 0.6 copy-done.6
  309.3 2.5 fusion.12
  312.0 0.6 copy-done.8
  312.6 2.4 fusion.13
  315.2 3.0 not_and_fusion
  318.2 0.8 slice.201
  319.3 0.8 slice.203
  320.6 1.0 iota_compare_fusion
  321.6 152.7 %all-to-all-done.1 = f32[6,2,512,512]{3,1,0,2:T(2,128)} async-done(((f32[6,2,512,512]{3,1,0,2:T(2,128)}), f32[6,2,512,512]{3,1,0,2:T(2,128)}, u32[]{:S(2)}, u32[]{:S(2)}) %all-to-all-start.1) | async-done | bytes 12582944 | tf_op jit(solution)/shard_map/all_to_all | solution.py:41
  474.3 13.1 %copy.17 = f32[6,2,512,512]{3,2,1,0:T(8,128)} copy(f32[6,2,512,512]{3,1,0,2:T(2,128)} %all-to-all-done.1) | data formatting | bytes 25165824 | tf_op jit(solution)/shard_map/all_to_all | solution.py:41
  487.4 11.3 %copy.22 = f32[6,2,8,8,8,512]{5,4,2,3,1,0:T(8,128)} copy(f32[6,2,8,8,8,512]{5,4,3,2,1,0:T(8,128)} %bitcast.22) | data formatting | bytes 25165824 | tf_op jit(solution)/shard_map/all_to_all | solution.py:41
  498.8 11.4 %broadcast_select_fusion = f32[6,2,64,4096]{3,2,1,0:T(8,128)} fusion(f32[6,2,64,4096]{3,2,1,0:T(8,128)} %bitcast.18, pred[2,64,4096]{2,1,0:T(8,128)(4,1)S(1)} %get-tuple-element.45), kind=kLoop, calls=%fused_computation.17 | loop fusion | flops 3145728 | bytes 25690112 | tf_op jit(solution)/shard_map/jit(_where)/select_n | solution.py:20
  510.2 12.5 %slice.189 = f32[6,2,64,4095]{3,2,1,0:T(8,128)} slice(f32[6,2,64,4096]{3,2,1,0:T(8,128)} %broadcast_select_fusion), slice={[0:6], [0:2], [0:64], [1:4096]} | slice | bytes 25159680 | tf_op jit(solution)/shard_map/slice | solution.py:11
  522.7 15.1 %select_select_fusion.10 = f32[6,2,64,4096]{3,2,1,0:T(8,128)} fusion(f32[6,2,64,4095]{3,2,1,0:T(8,128)} %slice.189, pred[2,64,4096]{2,1,0:T(8,128)(4,1)S(1)} %get-tuple-element.42, pred[2,64,4096]{2,1,0:T(8,128)(4,1)S(1)} %copy-done.10, f32[6,2,64,4096]{3,2,1,0:T(8,128)} %bitcast.19, pred[2,64,4096]{2,1,0:T(8,128)(4,1)S(1)} %get-tuple-element.45), kind=kLoop, calls=%fused_computation.10 | loop fusion | flops 9437184 | bytes 39318528 | tf_op jit(solution)/shard_map/jit(_where)/select_n | solution.py:28
  537.9 12.5 %slice.190 = f32[6,2,64,4094]{3,2,1,0:T(8,128)} slice(f32[6,2,64,4096]{3,2,1,0:T(8,128)} %select_select_fusion.10), slice={[0:6], [0:2], [0:64], [2:4096]} | slice | bytes 25153536 | tf_op jit(solution)/shard_map/slice | solution.py:11
  550.3 14.5 %select_select_fusion.9 = f32[6,2,64,4096]{3,2,1,0:T(8,128)} fusion(f32[6,2,64,4096]{3,2,1,0:T(8,128)} %select_select_fusion.10, f32[6,2,64,4094]{3,2,1,0:T(8,128)} %slice.190, pred[2,64,4096]{2,1,0:T(8,128)(4,1)S(1)} %get-tuple-element.39, pred[2,64,4096]{2,1,0:T(8,128)(4,1)S(1)} %copy-done.11), kind=kLoop, calls=%fused_computation.9 | loop fusion | flops 6291456 | bytes 38791168 | tf_op jit(solution)/shard_map/jit(_where)/select_n | solution.py:28
  564.8 12.5 %slice.191 = f32[6,2,64,4092]{3,2,1,0:T(8,128)} slice(f32[6,2,64,4096]{3,2,1,0:T(8,128)} %select_select_fusion.9), slice={[0:6], [0:2], [0:64], [4:4096]} | slice | bytes 25141248 | tf_op jit(solution)/shard_map/slice | solution.py:11
  577.2 14.6 %select_select_fusion.8 = f32[6,2,64,4096]{3,2,1,0:T(8,128)} fusion(f32[6,2,64,4096]{3,2,1,0:T(8,128)} %select_select_fusion.9, f32[6,2,64,4092]{3,2,1,0:T(8,128)} %slice.191, pred[2,64,4096]{2,1,0:T(8,128)(4,1)S(1)} %get-tuple-element.36, pred[2,64,4096]{2,1,0:T(8,128)(4,1)S(1)} %copy-done.12), kind=kLoop, calls=%fused_computation.8 | loop fusion | flops 6291456 | bytes 38785024 | tf_op jit(solution)/shard_map/jit(_where)/select_n | solution.py:28
  591.9 12.5 %slice.192 = f32[6,2,64,4088]{3,2,1,0:T(8,128)} slice(f32[6,2,64,4096]{3,2,1,0:T(8,128)} %select_select_fusion.8), slice={[0:6], [0:2], [0:64], [8:4096]} | slice | bytes 25116672 | tf_op jit(solution)/shard_map/slice | solution.py:11
  604.3 14.5 %select_select_fusion.7 = f32[6,2,64,4096]{3,2,1,0:T(8,128)} fusion(f32[6,2,64,4096]{3,2,1,0:T(8,128)} %select_select_fusion.8, f32[6,2,64,4088]{3,2,1,0:T(8,128)} %slice.192, pred[2,64,4096]{2,1,0:T(8,128)(4,1)S(1)} %get-tuple-element.33, pred[2,64,4096]{2,1,0:T(8,128)(4,1)S(1)} %copy-done.13), kind=kLoop, calls=%fused_computation.7 | loop fusion | flops 6291456 | bytes 38772736 | tf_op jit(solution)/shard_map/jit(_where)/select_n | solution.py:28
  618.8 12.5 %slice.193 = f32[6,2,64,4080]{3,2,1,0:T(8,128)} slice(f32[6,2,64,4096]{3,2,1,0:T(8,128)} %select_select_fusion.7), slice={[0:6], [0:2], [0:64], [16:4096]} | slice | bytes 25067520 | tf_op jit(solution)/shard_map/slice | solution.py:11
  631.3 14.7 %select_select_fusion.6 = f32[6,2,64,4096]{3,2,1,0:T(8,128)} fusion(f32[6,2,64,4096]{3,2,1,0:T(8,128)} %select_select_fusion.7, f32[6,2,64,4080]{3,2,1,0:T(8,128)} %slice.193, pred[2,64,4096]{2,1,0:T(8,128)(4,1)S(1)} %get-tuple-element.30, pred[2,64,4096]{2,1,0:T(8,128)(4,1)S(1)} %copy-done.14), kind=kLoop, calls=%fused_computation.6 | loop fusion | flops 6291456 | bytes 38748160 | tf_op jit(solution)/shard_map/jit(_where)/select_n | solution.py:28
  646.0 12.5 %slice.194 = f32[6,2,64,4064]{3,2,1,0:T(8,128)} slice(f32[6,2,64,4096]{3,2,1,0:T(8,128)} %select_select_fusion.6), slice={[0:6], [0:2], [0:64], [32:4096]} | slice | bytes 24969216 | tf_op jit(solution)/shard_map/slice | solution.py:11
  658.5 14.5 %select_select_fusion.5 = f32[6,2,64,4096]{3,2,1,0:T(8,128)} fusion(f32[6,2,64,4096]{3,2,1,0:T(8,128)} %select_select_fusion.6, f32[6,2,64,4064]{3,2,1,0:T(8,128)} %slice.194, pred[2,64,4096]{2,1,0:T(8,128)(4,1)S(1)} %copy-done.3, pred[2,64,4096]{2,1,0:T(8,128)(4,1)S(1)} %copy-done.15), kind=kLoop, calls=%fused_computation.5 | loop fusion | flops 6291456 | bytes 38699008 | tf_op jit(solution)/shard_map/jit(_where)/select_n | solution.py:28
  673.0 12.5 %slice.195 = f32[6,2,64,4032]{3,2,1,0:T(8,128)} slice(f32[6,2,64,4096]{3,2,1,0:T(8,128)} %select_select_fusion.5), slice={[0:6], [0:2], [0:64], [64:4096]} | slice | bytes 24772608 | tf_op jit(solution)/shard_map/slice | solution.py:11
  685.5 14.5 %select_select_fusion.4 = f32[6,2,64,4096]{3,2,1,0:T(8,128)} fusion(f32[6,2,64,4096]{3,2,1,0:T(8,128)} %select_select_fusion.5, f32[6,2,64,4032]{3,2,1,0:T(8,128)} %slice.195, pred[2,64,4096]{2,1,0:T(8,128)(4,1)S(1)} %copy-done.5, pred[2,64,4096]{2,1,0:T(8,128)(4,1)S(1)} %copy-done.16), kind=kLoop, calls=%fused_computation.4 | loop fusion | flops 6291456 | bytes 38600704 | tf_op jit(solution)/shard_map/jit(_where)/select_n | solution.py:28
  700.0 9.9 %slice.196 = f32[6,2,64,3968]{3,2,1,0:T(8,128)} slice(f32[6,2,64,4096]{3,2,1,0:T(8,128)} %select_select_fusion.4), slice={[0:6], [0:2], [0:64], [128:4096]} | slice | bytes 24379392 | tf_op jit(solution)/shard_map/slice | solution.py:11
  709.9 14.2 %select_select_fusion.3 = f32[6,2,64,4096]{3,2,1,0:T(8,128)} fusion(f32[6,2,64,4096]{3,2,1,0:T(8,128)} %select_select_fusion.4, f32[6,2,64,3968]{3,2,1,0:T(8,128)} %slice.196, pred[2,64,4096]{2,1,0:T(8,128)(4,1)S(1)} %copy-done.7, pred[2,64,4096]{2,1,0:T(8,128)(4,1)S(1)} %copy-done.17), kind=kLoop, calls=%fused_computation.3 | loop fusion | flops 6291456 | bytes 38404096 | tf_op jit(solution)/shard_map/jit(_where)/select_n | solution.py:28
  724.1 9.4 %slice.197 = f32[6,2,64,3840]{3,2,1,0:T(8,128)} slice(f32[6,2,64,4096]{3,2,1,0:T(8,128)} %select_select_fusion.3), slice={[0:6], [0:2], [0:64], [256:4096]} | slice | bytes 23592960 | tf_op jit(solution)/shard_map/slice | solution.py:11
  733.5 9.7 %select_select_fusion.2 = f32[6,2,64,4096]{3,2,1,0:T(8,128)S(1)} fusion(f32[6,2,64,4096]{3,2,1,0:T(8,128)} %select_select_fusion.3, f32[6,2,64,3840]{3,2,1,0:T(8,128)} %slice.197, pred[2,64,4096]{2,1,0:T(8,128)(4,1)} %copy-done.8, pred[2,64,4096]{2,1,0:T(8,128)(4,1)} %get-tuple-element.55), kind=kLoop, calls=%fused_computation.2 | loop fusion | flops 6291456 | bytes 38010880 | tf_op jit(solution)/shard_map/jit(_where)/select_n | solution.py:28
  743.2 5.2 slice.198
  748.4 10.8 %select_select_fusion.1 = f32[6,2,64,4096]{3,2,1,0:T(8,128)} fusion(f32[6,2,64,4096]{3,2,1,0:T(8,128)S(1)} %select_select_fusion.2, f32[6,2,64,3584]{3,2,1,0:T(8,128)} %slice.198, pred[2,64,4096]{2,1,0:T(8,128)(4,1)} %copy-done.9, pred[2,64,4096]{2,1,0:T(8,128)(4,1)} %get-tuple-element.56), kind=kLoop, calls=%fused_computation.1 | loop fusion | flops 6291456 | bytes 37224448 | tf_op jit(solution)/shard_map/jit(_where)/select_n | solution.py:28
  759.2 3.7 slice-done
  762.9 12.3 %select_select_fusion = f32[6,2,64,4096]{3,2,1,0:T(8,128)} fusion(f32[6,2,64,4096]{3,2,1,0:T(8,128)} %select_select_fusion.1, f32[6,2,64,3072]{3,2,1,0:T(8,128)S(1)} %slice-done, pred[2,64,4096]{2,1,0:T(8,128)(4,1)S(1)} %copy-done.18, pred[2,64,4096]{2,1,0:T(8,128)(4,1)} %get-tuple-element.57), kind=kLoop, calls=%fused_computation | loop fusion | flops 6291456 | bytes 35651584 | tf_op jit(solution)/shard_map/jit(_where)/select_n | solution.py:28
  775.3 2.7 slice-done.1
  778.3 10.7 %multiply_reduce_fusion = (f32[6,2]{1,0:T(8,128)S(1)}, f32[6,2,64,3072]{3,2,1,0:T(8,128)}) fusion(f32[6,2,64,4096]{3,2,1,0:T(8,128)} %select_select_fusion, pred[2,64,3072]{2,1,0:T(8,128)(4,1)S(1)} %copy-done.19, f32[6,2,64,2048]{3,2,1,0:T(8,128)S(1)} %slice-done.1, pred[2,64,3072]{2,1,0:T(8,128)(4,1)S(1)} %copy-done.20, f32[6,2,64,3072]{3,2,1,0:T(8,128)S(1)} %bitcast.24, ...), kind=kLoop, calls=%fused_computation.16 | loop fusion | flops 18874356 | bytes 35782704 | tf_op jit(solution)/shard_map/reduce_sum | solution.py:54
  789.0 19.7 %all-reduce.35 = (f32[6,2]{1,0:T(8,128)S(1)}, f32[2]{0:T(128)S(1)}) all-reduce(f32[6,2]{1,0:T(8,128)S(1)} %get-tuple-element.8, f32[2]{0:T(128)S(1)} %copy-done.22), channel_id=1, replica_groups=mesh['io'=8,'cmp'=4] {'io'}, use_global_device_ids=true, to_apply=%region_4.5 | all-reduce | flops 14 | bytes 112 | tf_op jit(solution)/shard_map/psum | solution.py:56
  808.8 0.7 copy.19
  (75 shorter events, 8.2 us)
Async XLA Ops:
  194.3 7.4 copy-start
  194.3 280.0 %all-to-all-start.1 = ((f32[6,2,512,512]{3,1,0,2:T(2,128)}), f32[6,2,512,512]{3,1,0,2:T(2,128)}, u32[]{:S(2)}, u32[]{:S(2)}) async-start(f32[6,2,512,512]{3,1,0,2:T(2,128)} %copy.16), calls=%async_computation.1 | async-start | bytes 25165824 | tf_op jit(solution)/shard_map/all_to_all | solution.py:41
  274.7 2.9 copy-start.1
  301.5 1.2 copy-start.2
  305.2 0.8 copy-start.4
  308.5 0.8 copy-start.6
  311.8 0.8 copy-start.8
  315.0 3.2 copy-start.9
  510.2 12.5 %copy-start.10 = (pred[2,64,4096]{2,1,0:T(8,128)(4,1)S(1)}, pred[2,64,4096]{2,1,0:T(8,128)(4,1)}, u32[]{:S(2)}) copy-start(pred[2,64,4096]{2,1,0:T(8,128)(4,1)} %get-tuple-element.53) | copy-start | bytes 1572868
  537.9 12.5 %copy-start.11 = (pred[2,64,4096]{2,1,0:T(8,128)(4,1)S(1)}, pred[2,64,4096]{2,1,0:T(8,128)(4,1)}, u32[]{:S(2)}) copy-start(pred[2,64,4096]{2,1,0:T(8,128)(4,1)} %get-tuple-element.52) | copy-start | bytes 1572868
  564.8 12.5 %copy-start.12 = (pred[2,64,4096]{2,1,0:T(8,128)(4,1)S(1)}, pred[2,64,4096]{2,1,0:T(8,128)(4,1)}, u32[]{:S(2)}) copy-start(pred[2,64,4096]{2,1,0:T(8,128)(4,1)} %get-tuple-element.51) | copy-start | bytes 1572868
  591.9 12.5 %copy-start.13 = (pred[2,64,4096]{2,1,0:T(8,128)(4,1)S(1)}, pred[2,64,4096]{2,1,0:T(8,128)(4,1)}, u32[]{:S(2)}) copy-start(pred[2,64,4096]{2,1,0:T(8,128)(4,1)} %get-tuple-element.50) | copy-start | bytes 1572868
  618.8 12.5 %copy-start.14 = (pred[2,64,4096]{2,1,0:T(8,128)(4,1)S(1)}, pred[2,64,4096]{2,1,0:T(8,128)(4,1)}, u32[]{:S(2)}) copy-start(pred[2,64,4096]{2,1,0:T(8,128)(4,1)} %get-tuple-element.49) | copy-start | bytes 1572868
  645.9 12.5 %copy-start.3 = (pred[2,64,4096]{2,1,0:T(8,128)(4,1)S(1)}, pred[2,64,4096]{2,1,0:T(8,128)(4,1)}, u32[]{:S(2)}) copy-start(pred[2,64,4096]{2,1,0:T(8,128)(4,1)} %copy-done.2) | copy-start | bytes 1572868
  646.0 12.5 %copy-start.15 = (pred[2,64,4096]{2,1,0:T(8,128)(4,1)S(1)}, pred[2,64,4096]{2,1,0:T(8,128)(4,1)}, u32[]{:S(2)}) copy-start(pred[2,64,4096]{2,1,0:T(8,128)(4,1)} %get-tuple-element.48) | copy-start | bytes 1572868
  673.0 12.5 %copy-start.5 = (pred[2,64,4096]{2,1,0:T(8,128)(4,1)S(1)}, pred[2,64,4096]{2,1,0:T(8,128)(4,1)}, u32[]{:S(2)}) copy-start(pred[2,64,4096]{2,1,0:T(8,128)(4,1)} %copy-done.4) | copy-start | bytes 1572868
  673.0 12.5 %copy-start.16 = (pred[2,64,4096]{2,1,0:T(8,128)(4,1)S(1)}, pred[2,64,4096]{2,1,0:T(8,128)(4,1)}, u32[]{:S(2)}) copy-start(pred[2,64,4096]{2,1,0:T(8,128)(4,1)} %get-tuple-element.47) | copy-start | bytes 1572868
  700.0 9.9 %copy-start.7 = (pred[2,64,4096]{2,1,0:T(8,128)(4,1)S(1)}, pred[2,64,4096]{2,1,0:T(8,128)(4,1)}, u32[]{:S(2)}) copy-start(pred[2,64,4096]{2,1,0:T(8,128)(4,1)} %copy-done.6) | copy-start | bytes 1572868
  700.0 9.9 %copy-start.17 = (pred[2,64,4096]{2,1,0:T(8,128)(4,1)S(1)}, pred[2,64,4096]{2,1,0:T(8,128)(4,1)}, u32[]{:S(2)}) copy-start(pred[2,64,4096]{2,1,0:T(8,128)(4,1)} %get-tuple-element.54) | copy-start | bytes 1572868
  759.2 3.7 slice-start
  759.2 3.7 copy-start.18
  759.2 16.1 %slice-start.2 = ((s8[9437184]{0:T(1024)(128)(4,1)}), s8[4194304]{0:T(1024)(128)(4,1)S(1)}, s32[]{:S(2)}) async-start(s8[9437184]{0:T(1024)(128)(4,1)} %bitcast.23), calls=%async_computation.4 | async-start | bytes 8388608
  762.9 12.4 %slice-start.3 = ((s8[9437184]{0:T(1024)(128)(4,1)}), s8[4194304]{0:T(1024)(128)(4,1)S(1)}, s32[]{:S(2)}) async-start(s8[9437184]{0:T(1024)(128)(4,1)} %bitcast.23), calls=%async_computation.5 | async-start | bytes 8388608
  762.9 12.4 %slice-start.4 = ((s8[9437184]{0:T(1024)(128)(4,1)}), s8[1048576]{0:T(1024)(128)(4,1)S(1)}, s32[]{:S(2)}) async-start(s8[9437184]{0:T(1024)(128)(4,1)} %bitcast.23), calls=%async_computation.6 | async-start | bytes 2097152
  775.2 2.8 slice-start.1
  775.2 2.8 copy-start.19
  775.2 2.9 copy-start.20
  775.2 3.0 copy-start.21
  778.3 10.7 %copy-start.22 = (f32[2]{0:T(128)S(1)}, f32[2]{0:T(128)}, u32[]{:S(2)}) copy-start(f32[2]{0:T(128)} %convert_element_type.2) | copy-start | bytes 28
where the time goes:
time: 819 us; the launch traced here: 810 us
  other arithmetic  270 us (33%)
  local copies, waits for them, and re-layouts  211 us (26%)
  blocking collectives  168 us (21%)
  waiting for transfers between devices  153 us (19%)
    all_to_all x1, waiting for transfers between devices, on_device(): lax.all_to_all(lax.all_to_all(fields, 'cmp', split_axis=1, concat_axis=2,...  153 us
    select_n x11, other arithmetic, pack_block(): jnp.where(arrive[None], move_left(values, amount), jnp.where(staying[None...  149 us
    all_to_all x1, blocking collectives, on_device(): lax.all_to_all(fields, 'cmp', split_axis=1, concat_axis=2, tiled=True)  148 us
    slice x37, local copies, waits for them, and re-layouts, move_left(): return jnp.concatenate([array[..., amount:], tail], axis=-1)  127 us
    another operation x3, other arithmetic  66.4 us
    all_to_all x2, local copies, waits for them, and re-layouts, on_device(): lax.all_to_all(fields, 'cmp', split_axis=1, concat_axis=2, tiled=True)  33.9 us
    and x11, other arithmetic, pack_block(): moving = present & (offset >> section & 1 == 1)  26.4 us
    all_to_all x2, local copies, waits for them, and re-layouts, on_device(): lax.all_to_all(lax.all_to_all(fields, 'cmp', split_axis=1, concat_axis=2,...  24.5 us
  transfers between devices with their start and end apart: 1, of which 1 were waited for; matrix products, arithmetic and copies ran while one was open for 15% of the time, Pallas kernels for 0%

commit v1 on v0

v1 whole, which is shorter than its diff:
```python
import functools

import jax
import jax.numpy as jnp
from jax import lax
from jax.experimental import pallas as pl
from jax.experimental.pallas import tpu as pltpu
from jax.sharding import PartitionSpec as P

STEPS = 3
LANES = 128
SUBS = 8
MESH = pl.DeviceIdType.MESH


def stages_of(count):
    return max(1, (count - 1).bit_length())


def lane_gather(array, index):
    return jnp.take_along_axis(array, index, axis=1, mode="promise_in_bounds")


def tile_rows(array):
    return jnp.concatenate(
        [array[:, t * LANES : (t + 1) * LANES] for t in range(array.shape[1] // LANES)], axis=0
    )


def tables(mask):
    rows = mask.shape[0]
    tiles = rows // SUBS
    lane = lax.broadcasted_iota(jnp.int32, (rows, LANES), 1)
    ranked = mask
    step = 1
    while step < LANES:
        ranked = ranked + jnp.where(lane >= step, pltpu.roll(ranked, step, 1), 0)
        step *= 2
    totals = jnp.broadcast_to(ranked[:, LANES - 1 :], (rows, LANES))
    bases = []
    base = jnp.zeros((SUBS, LANES), jnp.int32)
    for t in range(tiles):
        bases.append(base)
        base = base + totals[t * SUBS : (t + 1) * SUBS]
    counts = base
    base = jnp.concatenate(bases, axis=0)
    shift = jnp.where(mask == 1, lane - (ranked - 1), 0)
    step = 1
    while step < LANES:
        coming = pltpu.roll(shift, LANES - step, 1)
        shift = jnp.where(
            (coming & step) != 0, coming, jnp.where((shift & step) != 0, 0, shift)
        )
        step *= 2
    inside = (lane - base) & (LANES - 1)
    index = lane_gather((lane + shift) & (LANES - 1), inside)
    tile = lax.broadcasted_iota(jnp.int32, (rows, LANES), 0) // SUBS
    moves = jnp.where(inside < totals, tile - ((base + inside) >> 7), 0)
    bits = jnp.zeros((rows, LANES), jnp.int32)
    for k in range(stages_of(tiles)):
        amount = (1 << k) * SUBS
        if amount >= rows:
            break
        coming = jnp.concatenate(
            [moves[amount:], jnp.zeros((amount, LANES), jnp.int32)], axis=0
        )
        arrive = coming & (1 << k)
        bits = bits | arrive
        moves = jnp.where(
            arrive != 0, coming, jnp.where((moves & (1 << k)) != 0, 0, moves)
        )
    return index, bits, counts


def pack_rows(values, index, bits):
    rows = values.shape[0]
    tiles = rows // SUBS
    values = lane_gather(values, index)
    for k in range(stages_of(tiles)):
        amount = (1 << k) * SUBS
        if amount >= rows:
            break
        keep = rows - amount
        moved = jnp.where(
            (bits[:keep] & (1 << k)) != 0, values[amount:], values[:keep]
        )
        values = jnp.concatenate([moved, values[keep:]], axis=0)
    return values


def kernel(
    nio,
    ncmp,
    fields,
    mean_old,
    land_mask,
    mean_new,
    level_rms,
    recv,
    mean,
    mask,
    index,
    bits,
    counts,
    part,
    parts,
    send_sem,
    recv_sem,
    old_sem,
    new_sem,
    mask_sem,
    psend_sem,
    precv_sem,
):
    nfield, _, nlev, band, width = recv.shape
    width_out = mean.shape[-1]
    out_tiles = width_out // LANES
    groups = band // SUBS
    ratio = nio // ncmp
    ndest = ratio * ncmp
    my_io = lax.axis_index("io")
    my_cmp = lax.axis_index("cmp")

    def target(d):
        return ratio * my_cmp + lax.rem(d, ratio), lax.div(d, ratio)

    def piece(f, d):
        return fields.at[
            f,
            pl.ds(lax.div(d, ratio) * nlev, nlev),
            pl.ds(pl.multiple_of(lax.rem(d, ratio) * band, SUBS), band),
            :,
        ]

    def remote(f, d):
        to_io, to_cmp = target(d)
        return pltpu.make_async_remote_copy(
            src_ref=piece(f, d),
            dst_ref=recv.at[f, my_io],
            send_sem=send_sem.at[f, d],
            recv_sem=recv_sem.at[f, my_io],
            device_id=(to_io, to_cmp),
            device_id_type=MESH,
        )

    def local(f, d):
        return pltpu.make_async_copy(piece(f, d), recv.at[f, my_io], recv_sem.at[f, my_io])

    def is_me(d):
        to_io, to_cmp = target(d)
        return jnp.logical_and(to_io == my_io, to_cmp == my_cmp)

    def over_sends(action):
        def of_field(f, _):
            def of_dest(n, _):
                action(f, lax.rem(n + my_io, ndest))
                return 0

            return lax.fori_loop(0, ndest, of_dest, 0)

        lax.fori_loop(0, nfield, of_field, 0)

    def start(f, d):
        @pl.when(is_me(d))
        def _():
            local(f, d).start()

        @pl.when(jnp.logical_not(is_me(d)))
        def _():
            remote(f, d).start()

    def finish(f, d):
        @pl.when(jnp.logical_not(is_me(d)))
        def _():
            remote(f, d).wait_send()

    over_sends(start)

    mask_copy = pltpu.make_async_copy(land_mask, mask, mask_sem)
    mask_copy.start()

    def old_copy(f):
        return pltpu.make_async_copy(mean_old.at[f], mean.at[f], old_sem.at[f])

    def new_copy(f):
        return pltpu.make_async_copy(mean.at[f], mean_new.at[f], new_sem.at[f])

    def start_old(f, _):
        old_copy(f).start()
        return 0

    lax.fori_loop(0, nfield, start_old, 0)
    mask_copy.wait()
    part[...] = jnp.zeros(part.shape, jnp.float32)

    lane0 = lax.broadcasted_iota(jnp.int32, (SUBS, LANES), 1) == 0

    def rows_of(r):
        return pl.ds(pl.multiple_of(r * SUBS, SUBS), SUBS)

    for l in range(nlev):

        def make_tables(r, total, l=l):
            one_index, one_bits, one_counts = tables(tile_rows(mask[l, rows_of(r), :]))
            index[l, r] = one_index
            bits[l, r] = one_bits
            counts[l, r] = one_counts
            return total + one_counts

        total = lax.fori_loop(0, groups, make_tables, jnp.zeros((SUBS, LANES), jnp.int32))
        total = jnp.where(lane0, total, 0).astype(jnp.float32)
        row = nfield * nlev + l
        part[row : row + 1, :] = jnp.sum(total, axis=0, keepdims=True)

    def of_field(f, _):
        def arrived(s, _):
            pltpu.make_async_copy(recv.at[f, s], recv.at[f, s], recv_sem.at[f, s]).wait()
            return 0

        lax.fori_loop(0, nio, arrived, 0)
        old_copy(f).wait()
        slot = lax.broadcasted_iota(jnp.int32, (out_tiles * SUBS, LANES), 0)
        slot = (slot // SUBS) * LANES + lax.broadcasted_iota(
            jnp.int32, (out_tiles * SUBS, LANES), 1
        )

        for l in range(nlev):

            def of_rows(r, squares, l=l):
                at = rows_of(r)
                values = jnp.concatenate(
                    [tile_rows(recv[f, s, l, at, :]) for s in range(nio)], axis=0
                )
                packed = pack_rows(values, index[l, r], bits[l, r])[: out_tiles * SUBS]
                old = tile_rows(mean[f, l, at, :])
                in_row = slot < jnp.concatenate([counts[l, r]] * out_tiles, axis=0)
                new = jnp.where(
                    in_row, (STEPS * old + packed) * (1.0 / (STEPS + 1.0)), jnp.float32(0.0)
                )
                for t in range(out_tiles):
                    one = new[t * SUBS : (t + 1) * SUBS]
                    mean[f, l, at, t * LANES : (t + 1) * LANES] = one
                    squares = squares + one * one
                return squares

            squares = lax.fori_loop(0, groups, of_rows, jnp.zeros((SUBS, LANES), jnp.float32))
            part[pl.ds(f * nlev + l, 1), :] = jnp.sum(squares, axis=0, keepdims=True)
        new_copy(f).start()
        return 0

    lax.fori_loop(0, nfield, of_field, 0)
    parts[my_io] = part[...]
    over_sends(finish)

    def part_copy(p):
        return pltpu.make_async_remote_copy(
            src_ref=part,
            dst_ref=parts.at[my_io],
            send_sem=psend_sem.at[p],
            recv_sem=precv_sem.at[my_io],
            device_id=(lax.rem(my_io + p, nio), my_cmp),
            device_id_type=MESH,
        )

    def start_part(p, _):
        part_copy(p).start()
        return 0

    def finish_part(p, _):
        part_copy(p).wait_send()
        source = lax.rem(my_io + p, nio)
        pltpu.make_async_copy(parts.at[source], parts.at[source], precv_sem.at[source]).wait()
        return 0

    lax.fori_loop(1, nio, start_part, 0)
    lax.fori_loop(1, nio, finish_part, 0)

    summed = parts[0]
    for s in range(1, nio):
        summed = summed + parts[s]
    summed = jnp.sum(summed, axis=1, keepdims=True)
    for l in range(nlev):
        ocean_total = summed[nfield * nlev + l : nfield * nlev + l + 1]
        for f in range(nfield):
            one = summed[f * nlev + l : f * nlev + l + 1]
            level_rms[f : f + 1, l : l + 1] = jnp.sqrt(one / ocean_total + 1e-06)

    def finish_new(f, _):
        new_copy(f).wait()
        return 0

    lax.fori_loop(0, nfield, finish_new, 0)


def on_device(nio, ncmp, fields, mean_old, land_mask):
    nfield, nlev, band, width_out = mean_old.shape
    width = fields.shape[-1]
    ncol = land_mask.shape[-1]
    groups = band // SUBS
    rows = ncol // LANES * SUBS
    ndest = nio // ncmp * ncmp
    padded = -(-(nfield + 1) * nlev // SUBS) * SUBS
    dma = pltpu.SemaphoreType.DMA
    return pl.pallas_call(
        functools.partial(kernel, nio, ncmp),
        out_shape=(
            jax.ShapeDtypeStruct(mean_old.shape, jnp.float32),
            jax.ShapeDtypeStruct((nfield, nlev), jnp.float32),
        ),
        in_specs=[pl.BlockSpec(memory_space=pl.ANY)] * 3,
        out_specs=(
            pl.BlockSpec(memory_space=pl.ANY),
            pl.BlockSpec(memory_space=pltpu.VMEM),
        ),
        scratch_shapes=[
            pltpu.VMEM((nfield, nio, nlev, band, width), jnp.float32),
            pltpu.VMEM((nfield, nlev, band, width_out), jnp.float32),
            pltpu.VMEM((nlev, band, ncol), jnp.int32),
            pltpu.VMEM((nlev, groups, rows, LANES), jnp.int32),
            pltpu.VMEM((nlev, groups, rows, LANES), jnp.int32),
            pltpu.VMEM((nlev, groups, SUBS, LANES), jnp.int32),
            pltpu.VMEM((padded, LANES), jnp.float32),
            pltpu.VMEM((nio, padded, LANES), jnp.float32),
            dma((nfield, ndest)),
            dma((nfield, nio)),
            dma((nfield,)),
            dma((nfield,)),
            dma,
            dma((nio,)),
            dma((nio,)),
        ],
        compiler_params=pltpu.CompilerParams(has_side_effects=True),
    )(fields, mean_old, land_mask)


def solution(mesh):
    in_specs = (P(None, None, "cmp", "io"), P(None, "cmp", "io", None), P("cmp", "io", None))
    out_specs = (P(None, "cmp", "io", None), P(None, "cmp"))
    return jax.shard_map(
        functools.partial(on_device, mesh.shape["io"], mesh.shape["cmp"]),
        mesh=mesh,
        in_specs=in_specs,
        out_specs=out_specs,
        check_vma=False,
    )
```

time: 819 us -> 572 us (0.70); the launches traced: 810 us -> 572 us
  Pallas kernels: 0 us -> 561 us
  other arithmetic: 270 us -> 0 us
  local copies, waits for them, and re-layouts: 211 us -> 9.92 us
  blocking collectives: 168 us -> 0 us
  waiting for transfers between devices: 153 us -> 0 us
    pallas_call x0 -> x1, Pallas kernels: none -> 561 us  [on_device(): pl.pallas_call(functools.partial(kernel, nio, ncmp), out_shape=(jax.Shape...]
    select_n x12 -> x0, other arithmetic: 161 us -> none  [the longest x11 149 us: pack_block(): jnp.where(arrive[None], move_left(values, amount), jnp.where(staying[None...]
    all_to_all x1 -> x0, waiting for transfers between devices: 153 us -> none  [on_device(): lax.all_to_all(lax.all_to_all(fields, 'cmp', split_axis=1, concat_axis=2,...]
    all_to_all x1 -> x0, blocking collectives: 148 us -> none  [on_device(): lax.all_to_all(fields, 'cmp', split_axis=1, concat_axis=2, tiled=True)]
    slice x40 -> x0, local copies, waits for them, and re-layouts: 131 us -> none  [the longest x37 127 us: move_left(): return jnp.concatenate([array[..., amount:], tail], axis=-1)]
    another operation x3 -> x0, other arithmetic: 66.4 us -> none
    all_to_all x4 -> x0, local copies, waits for them, and re-layouts: 58.4 us -> none  [the longest x2 33.9 us: on_device(): lax.all_to_all(fields, 'cmp', split_axis=1, concat_axis=2, tiled=True)]
    and x12 -> x0, other arithmetic: 29.4 us -> none  [the longest x11 26.4 us: pack_block(): moving = present & (offset >> section & 1 == 1)]
  transfers between devices with their start and end apart: 1 -> 0, of which waited for: 1 -> 0; matrix products, arithmetic and copies ran while one was open for 15% -> 0% of each run, Pallas kernels for 0% -> 0%
where the time goes in v1:
time: 572 us
  Pallas kernels  561 us (98%)
  local copies, waits for them, and re-layouts  9.92 us (2%)
    pallas_call x1, Pallas kernels, on_device(): pl.pallas_call(functools.partial(kernel, nio, ncmp), out_shape=(jax.Shape...  561 us

profile of v1, /device:TPU:0, one launch (start us, length us, event | category | flops | bytes accessed | tf_op | source)
XLA Modules:
  0.0 572.0 jit_solution(8155924355879027198)
XLA Ops:
  0.6 561.5 %shard_map.50 = (f32[6,2,64,3072]{3,2,1,0:T(8,128)}, f32[6,2]{1,0:T(8,128)}) custom-call(f32[6,8,128,512]{3,2,1,0:T(8,128)} %fields.1, f32[6,2,64,3072]{3,2,1,0:T(8,128)} %mean_old.1, s32[2,64,4096]{2,1,0:T(8,128)} %land_mask.1), custom_call_target="tpu_custom_call" | custom-call | tf_op jit(solution)/shard_map/pallas_call | solution.py:304
  562.1 1.3 copy.5
  563.4 8.6 %copy.7 = f32[6,2,64,3072]{3,2,1,0:T(8,128)} copy(f32[6,2,64,3072]{3,2,1,0:T(8,128)} %get-tuple-element.6) | data formatting | bytes 18874368
